TPU v7x, 32 devices: a whole 2x2x4 slice. The times are simulated.
32 devices in a mesh: row: 8 (over y, x, core), col: 4 (over z).
Axes of the slice: x: 2, y: 2, z: 4, core: 2. Of those that a mesh axis runs over, the one named last changes fastest.
Arguments:
- alignment_state: bfloat16 [128, 128, 256], P('col', 'row'), may hold values from -6 to 6
- layer_norm_gain: float32 [256], replicated, may hold values from 0.1 to 1.9
- left_weight_matrix: bfloat16 [256, 32], replicated, may hold values from -0.375 to 0.375
- right_weight_matrix: bfloat16 [256, 32], replicated, may hold values from -0.375 to 0.375
- output_weight_matrix: bfloat16 [1024, 128], replicated, may hold values from -0.1875 to 0.1875
- output_bias_vector: float32 [128], replicated, may hold values from -3 to 3
- pair_update_cotangent: bfloat16 [128, 128, 128], P('row', 'col'), may hold values from -40 to 40
Outputs:
- pair_update_output: bfloat16 [128, 128, 128], P('row', 'col')
- alignment_gradient: bfloat16 [128, 128, 256], P('col', 'row')
- left_weight_gradient: float32 [256, 32], replicated
- right_weight_gradient: float32 [256, 32], replicated
- out_w_grad: float32 [1024, 128], P(('row', 'col'))
- norm_gain_gradient: float32 [256], replicated
- output_bias_gradient: float32 [128], replicated
All inputs are finite; a program needn't handle non-finite values.
Results may differ from a plain program's by a relative error of at most 0.024.
Values may be sent and summed in bfloat16 or wider, within the bound.
No kernel may reach another device: no remote copies, remote signals or barrier semaphores. Data moves between devices by JAX's collectives and lax.ppermute only.
A program may use at most 64 MiB of HBM per device.

v0:
```python
import jax
import jax.numpy as jnp
from jax import lax
from jax.sharding import PartitionSpec as P


def from_root(block, axis, holder):
    block = jnp.where(lax.axis_index(axis) == holder, block, jnp.zeros_like(block))
    return lax.psum(block, axis)


def apply_layer_norm(alignment_state):
    value_entries = alignment_state.astype(jnp.float32)
    center = value_entries - jnp.mean(value_entries, axis=-1, keepdims=True)
    inverse_deviation = lax.rsqrt(jnp.mean(center * center, axis=-1, keepdims=True) + 1e-05)
    return (center * inverse_deviation, inverse_deviation)


def on_device(
    alignment_state,
    layer_norm_gain,
    left_weight_matrix,
    right_weight_matrix,
    output_weight_matrix,
    output_bias_vector,
    pair_update_cotangent,
):
    sequence_block_local, residue_block_local, alignment_weight = alignment_state.shape
    proj_w = left_weight_matrix.shape[1]
    pair_w = output_weight_matrix.shape[1]
    row_count = lax.axis_size("row")
    col_count = lax.axis_size("col")
    row_ratio = row_count // col_count
    total_res = residue_block_local * row_count
    col_res = residue_block_local * row_ratio
    col_index = lax.axis_index("col")
    row_index = lax.axis_index("row")
    normed_alignment, inverse_deviation = apply_layer_norm(alignment_state)
    layer_norm_output = (normed_alignment * layer_norm_gain).astype(jnp.bfloat16)
    normed_flat_rows = layer_norm_output.reshape(-1, alignment_weight)
    left_local = (
        jnp.dot(normed_flat_rows, left_weight_matrix, preferred_element_type=jnp.float32)
        .astype(jnp.bfloat16)
        .reshape(sequence_block_local, residue_block_local, proj_w)
    )
    right_local = (
        jnp.dot(normed_flat_rows, right_weight_matrix, preferred_element_type=jnp.float32)
        .astype(jnp.bfloat16)
        .reshape(sequence_block_local, residue_block_local, proj_w)
    )
    left_all, right_rows = (
        lax.all_gather(left_local, "col", axis=0, tiled=True),
        lax.all_gather(right_local, "col", axis=0, tiled=True),
    )
    seq_total = left_all.shape[0]
    right_every = lax.all_gather(right_rows, "row", axis=1, tiled=True)
    right_block = lax.dynamic_slice_in_dim(right_every, col_index * col_res, col_res, 1)
    block_res = min(8, residue_block_local)

    def visit(totals, row_start):
        right_acc, projection_running_sum = totals
        left_part = lax.dynamic_slice_in_dim(left_all, row_start, block_res, 1)
        cot_part = lax.dynamic_slice_in_dim(pair_update_cotangent, row_start, block_res, 0)
        outer_prod = jnp.einsum(
            "sic,sjd->ijcd", left_part, right_block, preferred_element_type=jnp.float32
        )
        outer_flat = (
            (outer_prod / seq_total)
            .astype(jnp.bfloat16)
            .reshape(block_res * col_res, proj_w * proj_w)
        )
        cot_flat = cot_part.reshape(block_res * col_res, pair_w)
        pair_part = (
            jnp.dot(outer_flat, output_weight_matrix, preferred_element_type=jnp.float32)
            + output_bias_vector
        ).astype(jnp.bfloat16)
        projection_running_sum = projection_running_sum + lax.dot_general(
            outer_flat, cot_flat, (((0,), (0,)), ((), ())), preferred_element_type=jnp.float32
        )
        outer_grad = lax.dot_general(
            cot_flat,
            output_weight_matrix,
            (((1,), (1,)), ((), ())),
            preferred_element_type=jnp.float32,
        ).astype(jnp.bfloat16)
        outer_grad = outer_grad.reshape(block_res, col_res, proj_w, proj_w)
        left_part_grad = (
            jnp.einsum("ijcd,sjd->sic", outer_grad, right_block, preferred_element_type=jnp.float32)
            / seq_total
        )
        right_acc = (
            right_acc
            + jnp.einsum("ijcd,sic->sjd", outer_grad, left_part, preferred_element_type=jnp.float32)
            / seq_total
        )
        return (
            (right_acc, projection_running_sum),
            (pair_part.reshape(block_res, col_res, pair_w), left_part_grad),
        )

    starts = jnp.arange(residue_block_local // block_res, dtype=jnp.int32) * block_res
    initial = (
        jnp.zeros((seq_total, col_res, proj_w), jnp.float32),
        jnp.zeros((proj_w * proj_w, pair_w), jnp.float32),
    )
    (right_acc, projection_running_sum), (pair_parts, left_parts) = lax.scan(visit, initial, starts)
    pair_update_output = pair_parts.reshape(residue_block_local, col_res, pair_w)
    left_partial = jnp.transpose(left_parts, (1, 0, 2, 3)).reshape(
        seq_total, residue_block_local, proj_w
    )
    left_d = lax.psum_scatter(
        left_partial.astype(jnp.bfloat16), "col", scatter_dimension=0, tiled=True
    )
    right_full = lax.psum(right_acc.astype(jnp.bfloat16), "row").astype(jnp.float32)
    right_half = lax.dynamic_slice_in_dim(
        right_full, row_index % row_ratio * residue_block_local, residue_block_local, 1
    )
    right_home = from_root(right_half.astype(jnp.bfloat16), "col", row_index // row_ratio).astype(
        right_half.dtype
    )
    right_d = lax.dynamic_slice_in_dim(
        right_home, col_index * sequence_block_local, sequence_block_local, 0
    ).astype(jnp.bfloat16)
    left_flat = left_d.reshape(-1, proj_w)
    right_flat = right_d.reshape(-1, proj_w)
    normed_derivative = lax.dot_general(
        left_flat, left_weight_matrix, (((1,), (1,)), ((), ())), preferred_element_type=jnp.float32
    )
    normed_derivative = normed_derivative + lax.dot_general(
        right_flat,
        right_weight_matrix,
        (((1,), (1,)), ((), ())),
        preferred_element_type=jnp.float32,
    )
    normed_derivative = normed_derivative.reshape(
        sequence_block_local, residue_block_local, alignment_weight
    )
    scaled_product = normed_derivative * layer_norm_gain
    alignment_gradient = (
        (
            scaled_product
            - jnp.mean(scaled_product, axis=-1, keepdims=True)
            - normed_alignment * jnp.mean(scaled_product * normed_alignment, axis=-1, keepdims=True)
        )
        * inverse_deviation
    ).astype(jnp.bfloat16)
    weight_left = lax.dot_general(
        normed_flat_rows, left_flat, (((0,), (0,)), ((), ())), preferred_element_type=jnp.float32
    )
    weight_right = lax.dot_general(
        normed_flat_rows, right_flat, (((0,), (0,)), ((), ())), preferred_element_type=jnp.float32
    )
    gain_part = jnp.sum(normed_derivative * normed_alignment, axis=(0, 1))
    bias_part = jnp.sum(pair_update_cotangent, axis=(0, 1), dtype=jnp.float32)
    param_totals = lax.psum((weight_left, weight_right, gain_part, bias_part), ("row", "col"))
    proj_partial = lax.psum_scatter(
        projection_running_sum.astype(jnp.bfloat16), "row", scatter_dimension=0, tiled=True
    ).astype(jnp.float32)
    proj_total = lax.psum_scatter(proj_partial, "col", scatter_dimension=0, tiled=True)
    return (
        pair_update_output,
        alignment_gradient,
        param_totals[0] / total_res,
        param_totals[1] / total_res,
        proj_total / total_res,
        param_totals[2] / total_res,
        param_totals[3] / total_res,
    )


def solution(mesh):
    return jax.shard_map(
        on_device,
        mesh=mesh,
        in_specs=(P("col", "row", None), P(), P(), P(), P(), P(), P("row", "col", None)),
        out_specs=(
            P("row", "col", None),
            P("col", "row", None),
            P(),
            P(),
            P(("row", "col"), None),
            P(),
            P(),
        ),
        check_vma=False,
    )
```

profile of v0, /device:TPU:0, one launch (start us, length us, event | category | flops | bytes accessed | tf_op | source)
XLA Modules:
  0.0 416.1 jit_solution(7871246451103388164)
XLA Ops:
  7.2 1.1 convert_reduce_fusion
  8.4 1.2 fusion.27
  9.6 1.2 fusion.21
  11.1 18.0 %all_gather.10 = bf16[128,16,32]{2,1,0:T(8,128)(2,1)} all-gather(bf16[32,16,32]{2,1,0:T(8,128)(2,1)S(1)} %bitcast.126), channel_id=1, replica_groups=mesh['row'=8,'col'=4] {'col'}, dimensions={0}, use_global_device_ids=true | all-gather | bytes 163840 | tf_op jit(solution)/shard_map/all_gather | solution.py:53
  29.6 16.3 %all_gather.9 = bf16[128,16,32]{2,1,0:T(8,128)(2,1)S(1)} all-gather(bf16[32,16,32]{2,1,0:T(8,128)(2,1)S(1)} %bitcast.127), channel_id=1, replica_groups=mesh['row'=8,'col'=4] {'col'}, dimensions={0}, use_global_device_ids=true | all-gather | bytes 163840 | tf_op jit(solution)/shard_map/all_gather | solution.py:52
  46.8 21.7 %all-gather.2.cloned.1.call-done = bf16[128,128,32]{2,1,0:T(8,128)(2,1)} async-done(((bf16[128,16,32]{2,1,0:T(8,128)(2,1)}), bf16[128,128,32]{2,1,0:T(8,128)(2,1)}) %all-gather.2.cloned.1.call-update) | async-done | bytes 1048592 | tf_op jit(solution)/shard_map/all_gather | solution.py:56
  68.5 1.3 constant_dynamic-slice_fusion.1
  69.8 1.8 copy.44
  71.6 32.6 %while.17 = (s32[]{:T(128)}, f32[128,32,32]{0,2,1:T(8,128)}, f32[1024,128]{1,0:T(8,128)S(1)}, bf16[2,8,32,128]{3,2,1,0:T(8,128)(2,1)}, bf16[2,128,8,32]{1,3,2,0:...) while((s32[]{:T(128)}, f32[128,32,32]{0,2,1:T(8,128)}, ...), condition=%wide.region_3.4_spmd.clone, body=%wide.region_2.3_spmd.clone.sunk | while | flops 404193280 | bytes 15928666 | solution.py:106
  71.6 1.2 dynamic_slice.46
  74.8 1.7 fusion.79
  76.5 2.2 reshape.95
  78.7 0.9 constant_dynamic-slice_fusion.3
  80.0 0.8 copy-done.2
  81.1 1.6 reshape.94
  82.7 1.5 fusion.78
  84.6 0.6 copy-done.17
  85.3 2.1 fusion.81
  87.4 1.2 dynamic_slice.46
  90.6 1.7 fusion.79
  92.2 2.2 reshape.95
  94.5 0.9 constant_dynamic-slice_fusion.3
  95.8 0.8 copy-done.2
  96.9 1.6 reshape.94
  98.5 2.6 fusion.78
  101.5 0.6 copy-done.17
  102.1 2.1 fusion.81
  104.3 1.8 convert_element_type.67
  106.2 2.1 copy.45
  109.0 51.2 %all-reduce.5.cloned.1.call-done = bf16[128,32,32]{0,2,1:T(8,128)(2,1)} async-done(((bf16[128,32,32]{0,2,1:T(8,128)(2,1)}), bf16[128,32,32]{0,2,1:T(8,128)(2,1)}) %all-reduce.5.cloned.1.call-update) | async-done | bytes 262160 | tf_op jit(solution)/shard_map/psum | solution.py:114
  160.2 1.6 fusion.28
  161.8 21.9 %reduce-scatter.4.cloned.1.call-done = bf16[32,16,32]{2,1,0:T(8,128)(2,1)} async-done(((bf16[128,16,32]{2,1,0:T(8,128)(2,1)}), bf16[32,16,32]{2,1,0:T(8,128)(2,1)}) %reduce-scatter.4.cloned.1.call-update) | async-done | bytes 32784 | tf_op jit(solution)/shard_map/reduce_scatter | solution.py:111
  183.7 1.1 fusion.29
  184.8 1.7 convolution_bitcast_fusion.3
  186.5 32.9 %all-reduce.7.cloned.1.call-done = bf16[128,16,32]{0,2,1:T(8,128)(2,1)} async-done(((bf16[128,16,32]{0,2,1:T(8,128)(2,1)}), bf16[128,16,32]{0,2,1:T(8,128)(2,1)}) %all-reduce.7.cloned.1.call-update) | async-done | bytes 131088 | tf_op jit(solution)/shard_map/psum | solution.py:9
  219.4 1.0 convert_convert_fusion
  220.6 0.8 convolution_bitcast_fusion.2
  221.7 0.8 fusion.26
  222.6 0.7 convert_element_type.73
  223.5 1.0 fusion.25
  224.5 122.1 %all-reduce.9.cloned.1.call-done = (f32[256,32]{0,1:T(8,128)}, f32[256,32]{0,1:T(8,128)}, f32[256]{0:T(256)}, f32[128]{0:T(128)}) async-done(((f32[256,32]{0,1:T(8,128)}, f32[256,32]{0,1:T(8,128)}, f32[256]{0:T(256)}, f32[128]{0:T(128)}), (f32[256,32]{0,1:T(8,128)}, f32[256,32]{0,1:T(8,128)}, f32[256]{0:T(256)}, f32[128]{0:T(128)})) %all-reduce.9.cloned.1.call-update) | async-done | bytes 67088 | tf_op jit(solution)/shard_map/psum | solution.py:155
  346.7 1.2 broadcast_multiply_fusion.6
  347.9 1.4 broadcast_multiply_fusion
  349.3 37.1 %reduce-scatter.6.cloned.1.call-done = bf16[128,128]{1,0:T(8,128)(2,1)} async-done(((bf16[1024,128]{1,0:T(8,128)(2,1)}), bf16[128,128]{1,0:T(8,128)(2,1)}) %reduce-scatter.6.cloned.1.call-update) | async-done | bytes 32784 | tf_op jit(solution)/shard_map/reduce_scatter | solution.py:156
  386.4 1.4 convert_element_type.74
  387.8 1.1 broadcast_multiply_fusion.7
  388.9 19.1 %reduce-scatter.8.cloned.1.call-done = f32[32,128]{1,0:T(8,128)} async-done(((f32[128,128]{1,0:T(8,128)}), f32[32,128]{1,0:T(8,128)}) %reduce-scatter.8.cloned.1.call-update) | async-done | bytes 16400 | tf_op jit(solution)/shard_map/reduce_scatter | solution.py:159
  408.0 1.3 broadcast_multiply_fusion.2
  (82 shorter events, 5.4 us)
Async XLA Ops:
  7.2 3.6 copy-start
  7.2 22.1 %copy-start.12 = (bf16[256,32]{0,1:T(8,128)(2,1)S(1)}, bf16[256,32]{0,1:T(8,128)(2,1)}, u32[]{:S(2)}) copy-start(bf16[256,32]{0,1:T(8,128)(2,1)} %param.11) | copy-start | bytes 49156
  7.2 61.3 %all-gather.2.cloned.1.call-start = ((), (), s32[]{:S(2)}) async-start(), calls=%async_computation.3 | async-start | bytes 4718592 | tf_op jit(solution)/shard_map/all_gather | solution.py:56
  8.3 2.4 copy-start.8
  9.6 1.2 copy-start.10
  10.8 18.8 %copy-start.5 = (bf16[32,16,256]{2,1,0:T(8,128)(2,1)}, bf16[32,16,256]{2,1,0:T(8,128)(2,1)S(1)}, u32[]{:S(2)}) copy-start(bf16[32,16,256]{2,1,0:T(8,128)(2,1)S(1)} %fusion.21) | copy-start | bytes 786436
  29.1 131.0 %all-reduce.5.cloned.1.call-start = ((), (), s32[]{:S(2)}) async-start(), calls=%async_computation.5 | async-start | bytes 524288 | tf_op jit(solution)/shard_map/psum | solution.py:114
  45.9 25.7 %copy-start.1 = (bf16[1024,128]{1,0:T(8,128)(2,1)S(1)}, bf16[1024,128]{1,0:T(8,128)(2,1)}, u32[]{:S(2)}) copy-start(bf16[1024,128]{1,0:T(8,128)(2,1)} %param.13) | copy-start | bytes 786436
  80.0 0.8 copy-start.2
  82.7 1.6 copy-start.15
  82.7 1.9 copy-start.16
  84.3 3.1 copy-start.3
  84.6 0.7 copy-start.17
  95.8 0.8 copy-start.2
  98.5 2.7 copy-start.15
  98.5 2.9 copy-start.16
  101.1 3.1 copy-start.3
  101.5 0.7 copy-start.17
  104.2 4.1 copy-start.7
  104.2 79.5 %copy-start.13 = (bf16[256,32]{0,1:T(8,128)(2,1)S(1)}, bf16[256,32]{0,1:T(8,128)(2,1)}, u32[]{:S(2)}) copy-start(bf16[256,32]{0,1:T(8,128)(2,1)} %param.11) | copy-start | bytes 49156
  104.2 80.6 %copy-start.6 = (bf16[32,16,256]{2,1,0:T(8,128)(2,1)S(1)}, bf16[32,16,256]{2,1,0:T(8,128)(2,1)}, u32[]{:S(2)}) copy-start(bf16[32,16,256]{2,1,0:T(8,128)(2,1)} %copy-done.5) | copy-start | bytes 786436
  106.1 115.3 %copy-start.14 = (f32[256]{0:T(256)S(1)}, f32[256]{0:T(256)}, u32[]{:S(2)}) copy-start(f32[256]{0:T(256)} %param.10) | copy-start | bytes 3076
  106.1 77.6 %reduce-scatter.4.cloned.1.call-start = ((), (), s32[]{:S(2)}) async-start(), calls=%async_computation.4 | async-start | bytes 655360 | tf_op jit(solution)/shard_map/reduce_scatter | solution.py:111
  108.3 113.5 %copy-start.4 = (bf16[32,16,256]{2,1,0:T(8,128)(2,1)S(1)}, bf16[32,16,256]{2,1,0:T(8,128)(2,1)}, u32[]{:S(2)}) copy-start(bf16[32,16,256]{2,1,0:T(8,128)(2,1)} %param.9) | copy-start | bytes 786436
  108.3 113.5 %copy-start.9 = (f32[32,16]{1,0:T(8,128)S(1)}, f32[32,16]{1,0:T(8,128)}, u32[]{:S(2)}) copy-start(f32[32,16]{1,0:T(8,128)} %copy-done.8) | copy-start | bytes 6148
  108.3 113.5 %copy-start.11 = (f32[32,16]{1,0:T(8,128)S(1)}, f32[32,16]{1,0:T(8,128)}, u32[]{:S(2)}) copy-start(f32[32,16]{1,0:T(8,128)} %copy-done.10) | copy-start | bytes 6148
  108.3 111.1 %all-reduce.7.cloned.1.call-start = ((), (), s32[]{:S(2)}) async-start(), calls=%async_computation.6 | async-start | bytes 262144 | tf_op jit(solution)/shard_map/psum | solution.py:9
  161.8 184.9 %all-reduce.9.cloned.1.call-start = ((), (), s32[]{:S(2)}) async-start(), calls=%async_computation.9 | async-start | bytes 134144 | tf_op jit(solution)/shard_map/psum | solution.py:155
  222.5 163.9 %reduce-scatter.6.cloned.1.call-start = ((), (), s32[]{:S(2)}) async-start(), calls=%async_computation.7 | async-start | bytes 294912 | tf_op jit(solution)/shard_map/reduce_scatter | solution.py:156
  223.3 184.6 %reduce-scatter.8.cloned.1.call-start = ((), (), s32[]{:S(2)}) async-start(), calls=%async_computation.8 | async-start | bytes 81920 | tf_op jit(solution)/shard_map/reduce_scatter | solution.py:159
Sparse Core Ops, SparseCore 0:
  29.3 39.2 all-gather.1
  106.2 53.8 all-reduce.4
  162.4 21.2 reduce-scatter.3
  186.5 32.8 all-reduce.6
  225.9 120.6 all-reduce.8
  349.5 36.8 reduce-scatter.5
  388.6 19.2 reduce-scatter.7
where the time goes:
time: 417 us; the launch traced here: 416 us
  waiting for transfers between devices  306 us (73%)
  blocking collectives  34.3 us (8%)
  local copies, waits for them, and re-layouts  21 us (5%)
  matrix products  18.1 us (4%)
  other arithmetic  18 us (4%)
  between operations  14.4 us (3%)
    psum x1, waiting for transfers between devices, on_device(): lax.psum((weight_left, weight_right, gain_part, bias_part), ('row', 'col'))  122 us
    psum x1, waiting for transfers between devices, on_device(): lax.psum(right_acc.astype(jnp.bfloat16), 'row').astype(jnp.float32)  51.2 us
    reduce_scatter x1, waiting for transfers between devices, on_device(): lax.psum_scatter(projection_running_sum.astype(jnp.bfloat16), 'row', scat...  37.1 us
    psum x1, waiting for transfers between devices, from_root(): return lax.psum(block, axis)  32.9 us
    reduce_scatter x1, waiting for transfers between devices, on_device(): lax.psum_scatter(left_partial.astype(jnp.bfloat16), 'col', scatter_dimens...  21.9 us
    all_gather x1, waiting for transfers between devices, on_device(): right_every = lax.all_gather(right_rows, 'row', axis=1, tiled=True)  21.7 us
    reduce_scatter x1, waiting for transfers between devices, on_device(): lax.psum_scatter(proj_partial, 'col', scatter_dimension=0, tiled=True)  19.1 us
    all_gather x1, blocking collectives, on_device(): lax.all_gather(right_local, 'col', axis=0, tiled=True)  18 us
  transfers between devices with their start and end apart: 7, of which 7 were waited for; matrix products, arithmetic and copies ran while one was open for 3% of the time, Pallas kernels for 0%

commit v1 on v0

--- a/solution.py
+++ b/solution.py
@@ -152,7 +152,9 @@
     )
     gain_part = jnp.sum(normed_derivative * normed_alignment, axis=(0, 1))
     bias_part = jnp.sum(pair_update_cotangent, axis=(0, 1), dtype=jnp.float32)
-    param_totals = lax.psum((weight_left, weight_right, gain_part, bias_part), ("row", "col"))
+    param_totals = lax.psum(
+        lax.psum((weight_left, weight_right, gain_part, bias_part), "col"), "row"
+    )
     proj_partial = lax.psum_scatter(
         projection_running_sum.astype(jnp.bfloat16), "row", scatter_dimension=0, tiled=True
     ).astype(jnp.float32)

time: 417 us -> 380 us (0.911)
  waiting for transfers between devices: 306 us -> 269 us
    psum x1 -> x2, waiting for transfers between devices: 122 us -> 86.5 us  [the longest x1 52.4 us: on_device(): lax.psum(lax.psum((weight_left, weight_right, gain_part, bias_part), 'col...]
  transfers between devices with their start and end apart: 7 -> 8, of which waited for: 7 -> 8; matrix products, arithmetic and copies ran while one was open for 3% -> 4% of each run, Pallas kernels for 0% -> 0%
where the time goes in v1:
time: 380 us; the launch traced here: 379 us
  waiting for transfers between devices  269 us (71%)
  blocking collectives  34.3 us (9%)
  local copies, waits for them, and re-layouts  20.9 us (6%)
  matrix products  18.1 us (5%)
  other arithmetic  18 us (5%)
  between operations  14.4 us (4%)
  loops' own time  4.07 us (1%)
    psum x1, waiting for transfers between devices, on_device(): lax.psum(lax.psum((weight_left, weight_right, gain_part, bias_part), 'col...  52.4 us
    psum x1, waiting for transfers between devices, on_device(): lax.psum(right_acc.astype(jnp.bfloat16), 'row').astype(jnp.float32)  51.2 us
    reduce_scatter x1, waiting for transfers between devices, on_device(): lax.psum_scatter(projection_running_sum.astype(jnp.bfloat16), 'row', scat...  35.5 us
    psum x1, waiting for transfers between devices, on_device(): lax.psum((weight_left, weight_right, gain_part, bias_part), 'col')  34.2 us
    psum x1, waiting for transfers between devices, from_root(): return lax.psum(block, axis)  32.9 us
    reduce_scatter x1, waiting for transfers between devices, on_device(): lax.psum_scatter(left_partial.astype(jnp.bfloat16), 'col', scatter_dimens...  21.9 us
    all_gather x1, waiting for transfers between devices, on_device(): right_every = lax.all_gather(right_rows, 'row', axis=1, tiled=True)  21.7 us
    reduce_scatter x1, waiting for transfers between devices, on_device(): lax.psum_scatter(proj_partial, 'col', scatter_dimension=0, tiled=True)  19 us
  transfers between devices with their start and end apart: 8, of which 8 were waited for; matrix products, arithmetic and copies ran while one was open for 4% of the time, Pallas kernels for 0%

profile of v1, /device:TPU:0, one launch (start us, length us, event | category | flops | bytes accessed | tf_op | source)
XLA Modules:
  0.0 378.9 jit_solution(5912408314406808219)
XLA Ops:
  7.2 1.1 convert_reduce_fusion
  8.4 1.2 fusion.27
  9.6 1.2 fusion.21
  11.1 18.0 %all_gather.10 = bf16[128,16,32]{2,1,0:T(8,128)(2,1)} all-gather(bf16[32,16,32]{2,1,0:T(8,128)(2,1)S(1)} %bitcast.126), channel_id=1, replica_groups=mesh['row'=8,'col'=4] {'col'}, dimensions={0}, use_global_device_ids=true | all-gather | bytes 163840 | tf_op jit(solution)/shard_map/all_gather | solution.py:53
  29.6 16.3 %all_gather.9 = bf16[128,16,32]{2,1,0:T(8,128)(2,1)S(1)} all-gather(bf16[32,16,32]{2,1,0:T(8,128)(2,1)S(1)} %bitcast.127), channel_id=1, replica_groups=mesh['row'=8,'col'=4] {'col'}, dimensions={0}, use_global_device_ids=true | all-gather | bytes 163840 | tf_op jit(solution)/shard_map/all_gather | solution.py:52
  46.8 21.7 %all-gather.2.cloned.1.call-done = bf16[128,128,32]{2,1,0:T(8,128)(2,1)} async-done(((bf16[128,16,32]{2,1,0:T(8,128)(2,1)}), bf16[128,128,32]{2,1,0:T(8,128)(2,1)}) %all-gather.2.cloned.1.call-update) | async-done | bytes 1048592 | tf_op jit(solution)/shard_map/all_gather | solution.py:56
  68.5 1.3 constant_dynamic-slice_fusion.1
  69.8 1.8 copy.44
  71.6 32.6 %while.17 = (s32[]{:T(128)}, f32[128,32,32]{0,2,1:T(8,128)}, f32[1024,128]{1,0:T(8,128)S(1)}, bf16[2,8,32,128]{3,2,1,0:T(8,128)(2,1)}, bf16[2,128,8,32]{1,3,2,0:...) while((s32[]{:T(128)}, f32[128,32,32]{0,2,1:T(8,128)}, ...), condition=%wide.region_3.4_spmd.clone, body=%wide.region_2.3_spmd.clone.sunk | while | flops 404193280 | bytes 15928666 | solution.py:106
  71.6 1.2 dynamic_slice.46
  74.8 1.7 fusion.79
  76.5 2.2 reshape.95
  78.7 0.9 constant_dynamic-slice_fusion.3
  80.0 0.8 copy-done.2
  81.1 1.6 reshape.94
  82.7 1.5 fusion.78
  84.6 0.6 copy-done.17
  85.2 2.1 fusion.81
  87.4 1.2 dynamic_slice.46
  90.6 1.7 fusion.79
  92.2 2.2 reshape.95
  94.5 0.9 constant_dynamic-slice_fusion.3
  95.8 0.8 copy-done.2
  96.9 1.6 reshape.94
  98.5 2.6 fusion.78
  102.1 2.1 fusion.81
  104.2 1.8 convert_element_type.67
  106.1 2.1 copy.45
  108.9 51.2 %all-reduce.7.cloned.1.call-done = bf16[128,32,32]{0,2,1:T(8,128)(2,1)} async-done(((bf16[128,32,32]{0,2,1:T(8,128)(2,1)}), bf16[128,32,32]{0,2,1:T(8,128)(2,1)}) %all-reduce.7.cloned.1.call-update) | async-done | bytes 262160 | tf_op jit(solution)/shard_map/psum | solution.py:114
  160.1 1.6 fusion.28
  161.8 21.9 %reduce-scatter.4.cloned.1.call-done = bf16[32,16,32]{2,1,0:T(8,128)(2,1)} async-done(((bf16[128,16,32]{2,1,0:T(8,128)(2,1)}), bf16[32,16,32]{2,1,0:T(8,128)(2,1)}) %reduce-scatter.4.cloned.1.call-update) | async-done | bytes 32784 | tf_op jit(solution)/shard_map/reduce_scatter | solution.py:111
  183.7 1.1 fusion.29
  184.8 1.7 convolution_bitcast_fusion.3
  186.5 32.9 %all-reduce.9.cloned.1.call-done = bf16[128,16,32]{0,2,1:T(8,128)(2,1)} async-done(((bf16[128,16,32]{0,2,1:T(8,128)(2,1)}), bf16[128,16,32]{0,2,1:T(8,128)(2,1)}) %all-reduce.9.cloned.1.call-update) | async-done | bytes 131088 | tf_op jit(solution)/shard_map/psum | solution.py:9
  219.4 1.0 convert_convert_fusion
  220.5 0.8 convolution_bitcast_fusion.2
  221.7 0.8 fusion.26
  222.5 34.2 %all-reduce.13.cloned.1.call-done = (f32[256,32]{0,1:T(8,128)}, f32[256,32]{0,1:T(8,128)}, f32[256]{0:T(256)}, f32[128]{0:T(128)}) async-done(((f32[256,32]{0,1:T(8,128)}, f32[256,32]{0,1:T(8,128)}, f32[256]{0:T(256)}, f32[128]{0:T(128)}), (f32[256,32]{0,1:T(8,128)}, f32[256,32]{0,1:T(8,128)}, f32[256]{0:T(256)}, f32[128]{0:T(128)})) %all-reduce.13.cloned.1.call-update) | async-done | bytes 67088 | tf_op jit(solution)/shard_map/psum | solution.py:156
  256.8 0.7 convert_element_type.73
  257.7 1.0 fusion.25
  258.8 52.4 %all-reduce.11.cloned.1.call-done = (f32[256,32]{0,1:T(8,128)}, f32[256,32]{0,1:T(8,128)}, f32[256]{0:T(256)}, f32[128]{0:T(128)}) async-done(((f32[256,32]{0,1:T(8,128)}, f32[256,32]{0,1:T(8,128)}, f32[256]{0:T(256)}, f32[128]{0:T(128)}), (f32[256,32]{0,1:T(8,128)}, f32[256,32]{0,1:T(8,128)}, f32[256]{0:T(256)}, f32[128]{0:T(128)})) %all-reduce.11.cloned.1.call-update) | async-done | bytes 67088 | tf_op jit(solution)/shard_map/psum | solution.py:155
  311.1 1.2 broadcast_multiply_fusion.6
  312.3 1.4 broadcast_multiply_fusion
  313.8 35.5 %reduce-scatter.6.cloned.1.call-done = bf16[128,128]{1,0:T(8,128)(2,1)} async-done(((bf16[1024,128]{1,0:T(8,128)(2,1)}), bf16[128,128]{1,0:T(8,128)(2,1)}) %reduce-scatter.6.cloned.1.call-update) | async-done | bytes 32784 | tf_op jit(solution)/shard_map/reduce_scatter | solution.py:158
  349.2 1.4 convert_element_type.74
  350.6 1.1 broadcast_multiply_fusion.7
  351.7 19.0 %reduce-scatter.8.cloned.1.call-done = f32[32,128]{1,0:T(8,128)} async-done(((f32[128,128]{1,0:T(8,128)}), f32[32,128]{1,0:T(8,128)}) %reduce-scatter.8.cloned.1.call-update) | async-done | bytes 16400 | tf_op jit(solution)/shard_map/reduce_scatter | solution.py:161
  370.8 1.3 broadcast_multiply_fusion.2
  (85 shorter events, 6.1 us)
Async XLA Ops:
  7.2 3.6 copy-start
  7.2 22.1 %copy-start.12 = (bf16[256,32]{0,1:T(8,128)(2,1)S(1)}, bf16[256,32]{0,1:T(8,128)(2,1)}, u32[]{:S(2)}) copy-start(bf16[256,32]{0,1:T(8,128)(2,1)} %param.11) | copy-start | bytes 49156
  7.2 61.3 %all-gather.2.cloned.1.call-start = ((), (), s32[]{:S(2)}) async-start(), calls=%async_computation.3 | async-start | bytes 4718592 | tf_op jit(solution)/shard_map/all_gather | solution.py:56
  8.3 2.4 copy-start.8
  9.6 1.2 copy-start.10
  10.8 18.8 %copy-start.5 = (bf16[32,16,256]{2,1,0:T(8,128)(2,1)}, bf16[32,16,256]{2,1,0:T(8,128)(2,1)S(1)}, u32[]{:S(2)}) copy-start(bf16[32,16,256]{2,1,0:T(8,128)(2,1)S(1)} %fusion.21) | copy-start | bytes 786436
  29.1 131.0 %all-reduce.7.cloned.1.call-start = ((), (), s32[]{:S(2)}) async-start(), calls=%async_computation.5 | async-start | bytes 524288 | tf_op jit(solution)/shard_map/psum | solution.py:114
  45.9 25.7 %copy-start.1 = (bf16[1024,128]{1,0:T(8,128)(2,1)S(1)}, bf16[1024,128]{1,0:T(8,128)(2,1)}, u32[]{:S(2)}) copy-start(bf16[1024,128]{1,0:T(8,128)(2,1)} %param.13) | copy-start | bytes 786436
  80.0 0.8 copy-start.2
  82.7 1.6 copy-start.15
  82.7 1.8 copy-start.16
  84.3 3.1 copy-start.3
  84.6 0.7 copy-start.17
  95.8 0.8 copy-start.2
  98.5 2.6 copy-start.15
  98.5 2.9 copy-start.16
  101.1 3.1 copy-start.3
  101.4 0.7 copy-start.17
  104.2 4.1 %copy-start.7 = (bf16[16,32,128]{2,1,0:T(8,128)(2,1)S(1)}, bf16[16,32,128]{2,1,0:T(8,128)(2,1)}, u32[]{:S(2)}) copy-start(bf16[16,32,128]{2,1,0:T(8,128)(2,1)} %get-tuple-element.311) | copy-start | bytes 393220
  104.2 79.5 %copy-start.13 = (bf16[256,32]{0,1:T(8,128)(2,1)S(1)}, bf16[256,32]{0,1:T(8,128)(2,1)}, u32[]{:S(2)}) copy-start(bf16[256,32]{0,1:T(8,128)(2,1)} %param.11) | copy-start | bytes 49156
  104.2 80.6 %copy-start.6 = (bf16[32,16,256]{2,1,0:T(8,128)(2,1)S(1)}, bf16[32,16,256]{2,1,0:T(8,128)(2,1)}, u32[]{:S(2)}) copy-start(bf16[32,16,256]{2,1,0:T(8,128)(2,1)} %copy-done.5) | copy-start | bytes 786436
  106.1 115.3 %copy-start.14 = (f32[256]{0:T(256)S(1)}, f32[256]{0:T(256)}, u32[]{:S(2)}) copy-start(f32[256]{0:T(256)} %param.10) | copy-start | bytes 3076
  106.1 77.6 %reduce-scatter.4.cloned.1.call-start = ((), (), s32[]{:S(2)}) async-start(), calls=%async_computation.4 | async-start | bytes 655360 | tf_op jit(solution)/shard_map/reduce_scatter | solution.py:111
  108.2 113.4 %copy-start.4 = (bf16[32,16,256]{2,1,0:T(8,128)(2,1)S(1)}, bf16[32,16,256]{2,1,0:T(8,128)(2,1)}, u32[]{:S(2)}) copy-start(bf16[32,16,256]{2,1,0:T(8,128)(2,1)} %param.9) | copy-start | bytes 786436
  108.2 113.5 %copy-start.9 = (f32[32,16]{1,0:T(8,128)S(1)}, f32[32,16]{1,0:T(8,128)}, u32[]{:S(2)}) copy-start(f32[32,16]{1,0:T(8,128)} %copy-done.8) | copy-start | bytes 6148
  108.2 113.5 %copy-start.11 = (f32[32,16]{1,0:T(8,128)S(1)}, f32[32,16]{1,0:T(8,128)}, u32[]{:S(2)}) copy-start(f32[32,16]{1,0:T(8,128)} %copy-done.10) | copy-start | bytes 6148
  108.2 111.1 %all-reduce.9.cloned.1.call-start = ((), (), s32[]{:S(2)}) async-start(), calls=%async_computation.6 | async-start | bytes 262144 | tf_op jit(solution)/shard_map/psum | solution.py:9
  161.7 95.0 %all-reduce.13.cloned.1.call-start = ((), (), s32[]{:S(2)}) async-start(), calls=%async_computation.10 | async-start | bytes 134144 | tf_op jit(solution)/shard_map/psum | solution.py:156
  222.5 88.6 %all-reduce.11.cloned.1.call-start = ((), (), s32[]{:S(2)}) async-start(), calls=%async_computation.9 | async-start | bytes 134144 | tf_op jit(solution)/shard_map/psum | solution.py:155
  256.8 92.4 %reduce-scatter.6.cloned.1.call-start = ((), (), s32[]{:S(2)}) async-start(), calls=%async_computation.7 | async-start | bytes 294912 | tf_op jit(solution)/shard_map/reduce_scatter | solution.py:158
  257.6 113.2 %reduce-scatter.8.cloned.1.call-start = ((), (), s32[]{:S(2)}) async-start(), calls=%async_computation.8 | async-start | bytes 81920 | tf_op jit(solution)/shard_map/reduce_scatter | solution.py:161
Sparse Core Ops, SparseCore 0:
  29.3 39.2 all-gather.1
  106.2 53.8 all-reduce.6
  162.4 21.2 reduce-scatter.3
  186.4 32.8 all-reduce.8
  222.6 34.0 all-reduce.12
  260.1 50.9 all-reduce.10
  314.1 35.0 reduce-scatter.5
  351.5 19.2 reduce-scatter.7
